TPU v7x, 512 devices: a whole 4x8x8 slice. The times are simulated.
512 devices in a mesh: list: 32 (over y_hi, x, core), shard: 16 (over z, y_lo).
Axes of the slice: x: 4, y: 8 (y_hi: 4, y_lo: 2; y = y_hi * 2 + y_lo), z: 8, core: 2. Of those that a mesh axis runs over, the one named last changes fastest.
Arguments:
- features: bfloat16 [4096, 4096], P(('list', 'shard')), may hold values from -6 to 6
- norm_gain: float32 [4096], replicated, may hold values from 0.5 to 1.5
- gate_weight: bfloat16 [4096, 11008], P('shard', 'list'), may hold values from -0.09375 to 0.09375
- up_weight: bfloat16 [4096, 11008], P('shard', 'list'), may hold values from -0.09375 to 0.09375
- down_weight: bfloat16 [11008, 4096], P('list', 'shard'), may hold values from -0.0546875 to 0.0546875
- centroids: float32 [64, 4096], P('list'), may hold values from -6 to 6
- list_ids: int32 [4096], P(('list', 'shard')), may hold values from 0 to 63
- live: int32 [4096], P(('list', 'shard')), may hold values 0 or 1
Outputs:
- residuals: bfloat16 [4096, 4096], P(('list', 'shard'))
- refreshed: float32 [64, 4096], P('list')
All inputs are finite; a program needn't handle non-finite values. No bound on the sum of `live` on one device may be relied on, other than what follows from the above.
Results may differ from a plain program's by a relative error of at most 0.015.
Values may be sent and summed in bfloat16 or wider, within the bound.
No kernel may reach another device: no remote copies, remote signals or barrier semaphores. Data moves between devices by JAX's collectives and lax.ppermute only.
A program may use at most 64 MiB of HBM per device.

v0:
```python
import jax
import jax.numpy as jnp
from jax import lax
from jax.sharding import PartitionSpec as P


def laid_out(parts, dim):
    shape = list(parts.shape[1:])
    shape[dim] *= parts.shape[0]
    return jnp.moveaxis(parts, 0, dim).reshape(shape)


def from_everyone(value, axis):
    copies = jnp.broadcast_to(value, (lax.axis_size(axis), *value.shape))
    return lax.all_to_all(copies, axis, split_axis=0, concat_axis=0, tiled=True)


def collect(value, axis, dim):
    return laid_out(from_everyone(value, axis), dim)


def in_one_piece(arrays, axis, dim, along):
    both = jnp.concatenate(arrays, axis=along)
    filled, at, done = (lax.all_gather(both, axis, axis=dim, tiled=True), 0, [])
    for a in arrays:
        done.append(lax.slice_in_dim(filled, at, at + a.shape[along], axis=along))
        at += a.shape[along]
    return tuple(done)


def split_up(value, dim, peers):
    before, after = (value.shape[:dim], value.shape[dim + 1 :])
    return jnp.moveaxis(value.reshape(*before, peers, -1, *after), dim, 0)


def sum_at_owner(value, axis, dim):
    peers = lax.axis_size(axis)
    parts = lax.all_to_all(split_up(value, dim, peers), axis, 0, 0, tiled=True)
    return jnp.sum(parts.astype(jnp.float32), axis=0)


def sent_together(arrays, axis, dim, along):
    columns = [a.reshape(*a.shape[:along], -1) for a in arrays]
    both = jnp.concatenate(columns, axis=along)
    filled, at, done = (sum_at_owner(both, axis, dim), 0, [])
    for a, column in zip(arrays, columns):
        share = filled[..., at : at + column.shape[along]]
        done.append(share.reshape(*share.shape[:along], *a.shape[along:]))
        at += column.shape[along]
    return tuple(done)


def taken_together(value, axis):
    return from_everyone(value, axis).astype(jnp.float32).sum(axis=0)


def body(features, norm_gain, gate_weight, up_weight, down_weight, centroids, list_ids, live):
    group_rows = collect(features, "list", 0)
    pieces = in_one_piece((gate_weight, up_weight), "shard", 0, 1)
    first = jnp.dot(group_rows, pieces[0], preferred_element_type=jnp.float32)
    second = jnp.dot(group_rows, pieces[1], preferred_element_type=jnp.float32)
    hidden = (jax.nn.silu(first) * second).astype(jnp.bfloat16)
    partial_sums = jnp.dot(
        hidden,
        lax.all_gather(down_weight, "shard", axis=1, tiled=True),
        preferred_element_type=jnp.float32,
    )
    mixed = sum_at_owner(partial_sums.astype(jnp.bfloat16), "list", 0)
    stream = features.astype(jnp.float32) + mixed
    scale = lax.rsqrt(jnp.mean(stream * stream, axis=1, keepdims=True) + 1e-05)
    embedding = (stream * scale * norm_gain).astype(jnp.bfloat16)
    table = lax.all_gather(centroids.astype(jnp.bfloat16), "list", axis=0, tiled=True)
    list_total = table.shape[0]
    alive = live.astype(jnp.float32)
    member = (list_ids[:, None] == jnp.arange(list_total, dtype=jnp.int32)[None, :]).astype(
        jnp.float32
    )
    picked = jnp.dot(member.astype(jnp.bfloat16), table, preferred_element_type=jnp.float32)
    residuals = (alive[:, None] * (embedding.astype(jnp.float32) - picked)).astype(jnp.bfloat16)
    weighted = member * alive[:, None]
    dense_sums = jnp.dot(weighted.T, embedding.astype(jnp.float32), precision=lax.Precision.HIGHEST)
    dense_counts = jnp.sum(weighted, axis=0)
    owned_sums, owned_counts = sent_together(
        (dense_sums.astype(jnp.bfloat16), dense_counts.astype(jnp.bfloat16)), "list", 0, 1
    )
    total_sums, total_counts = (
        taken_together(owned_sums.astype(jnp.bfloat16), "shard").astype(jnp.float32),
        taken_together(owned_counts.astype(jnp.bfloat16), "shard").astype(jnp.float32),
    )
    refreshed = (centroids + total_sums) / (1.0 + total_counts[:, None])
    return (residuals, refreshed)


def solution(mesh):
    in_specs = (
        P(("list", "shard"), None),
        P(),
        P("shard", "list"),
        P("shard", "list"),
        P("list", "shard"),
        P("list", None),
        P(("list", "shard")),
        P(("list", "shard")),
    )
    out_specs = (P(("list", "shard"), None), P("list", None))
    return jax.shard_map(body, mesh=mesh, in_specs=in_specs, out_specs=out_specs, check_vma=False)
```

profile of v0, /device:TPU:1, one launch (start us, length us, event | category | flops | bytes accessed | tf_op | source)
XLA Modules:
  0.0 452.9 jit_solution(17762954597065309443)
XLA Ops:
  7.2 1.8 pad_maximum_fusion.1
  9.1 0.7 all-gather.6.cloned.1.call-update
  9.8 1.1 broadcast_in_dim.6
  10.9 81.3 %all_to_all.26 = bf16[32,8,4096]{2,1,0:T(8,128)(2,1)S(1)} all-to-all(bf16[32,8,4096]{2,1,0:T(8,128)(2,1)S(1)} %broadcast_in_dim.6), channel_id=1, replica_groups=mesh['list'=32,'shard'=16] {'list'}, dimensions={0} | all-to-all | bytes 4194304 | tf_op jit(solution)/shard_map/all_to_all | solution.py:15
  92.2 94.7 %all-gather.4.cloned.1.call-done = bf16[4096,688]{0,1:T(8,128)(2,1)} async-done(((bf16[256,688]{0,1:T(8,128)(2,1)}), bf16[4096,688]{0,1:T(8,128)(2,1)}) %all-gather.4.cloned.1.call-update) | async-done | bytes 5636112 | tf_op jit(solution)/shard_map/all_gather | solution.py:24
  186.9 2.9 fusion.9
  189.8 77.1 %all-gather.6.cloned.1.call-done = bf16[344,4096]{1,0:T(8,128)(2,1)} async-done(((bf16[344,256]{1,0:T(8,128)(2,1)}), bf16[344,4096]{1,0:T(8,128)(2,1)}) %all-gather.6.cloned.1.call-update) | async-done | bytes 2818064 | tf_op jit(solution)/shard_map/all_gather | solution.py:65
  266.9 7.7 %fusion = bf16[32,8,4096]{2,1,0:T(8,128)(2,1)} fusion(bf16[344,4096]{1,0:T(8,128)(2,1)} %all-gather.6.cloned.1.call-done, bf16[32,8,4096]{2,1,0:T(8,128)(2,1)S(1)} %all_to_all.26, bf16[4096,688]{0,1:T(8,128)(2,1)} %all-gather.4.cloned.1.call-done, f32[256,344]{0,1:T(8,128)S(1)} %fusion.9), kind=kOutput, calls=%fused_computation.1 | convolution fusion | flops 1444417536 | bytes 10182656 | tf_op jit(solution)/shard_map/dot_general | solution.py:63
  274.6 19.3 %all-to-all-start.1 = ((bf16[32,8,4096]{2,1,0:T(8,128)(2,1)}), bf16[32,8,4096]{2,1,0:T(8,128)(2,1)S(1)}, u32[]{:S(2)}, u32[]{:S(2)}) async-start(bf16[32,8,4096]{2,1,0:T(8,128)(2,1)} %fusion), calls=%async_computation.1 | async-start | bytes 4194304 | tf_op jit(solution)/shard_map/all_to_all | solution.py:38
  294.1 0.1 convert_element_type.84
  294.2 50.7 %all-to-all-done.1 = bf16[32,8,4096]{2,1,0:T(8,128)(2,1)S(1)} async-done(((bf16[32,8,4096]{2,1,0:T(8,128)(2,1)}), bf16[32,8,4096]{2,1,0:T(8,128)(2,1)S(1)}, u32[]{:S(2)}, u32[]{:S(2)}) %all-to-all-start.1) | async-done | bytes 2097184 | tf_op jit(solution)/shard_map/all_to_all | solution.py:38
  344.9 0.3 convert_reduce_fusion
  345.2 0.2 multiply_reduce_fusion
  345.5 0.7 convolution_convert_fusion.1
  346.2 0.3 concatenate.10
  346.5 0.5 pad_maximum_fusion
  347.1 23.8 %all_to_all.27 = bf16[32,2,4097]{2,1,0:T(2,128)(2,1)S(1)} all-to-all(bf16[32,2,4097]{2,1,0:T(2,128)(2,1)S(1)} %pad_maximum_fusion), channel_id=1, replica_groups=mesh['list'=32,'shard'=16] {'list'}, dimensions={0} | all-to-all | bytes 1048832 | tf_op jit(solution)/shard_map/all_to_all | solution.py:38
  370.9 0.4 reduce.1
  371.4 0.1 slice_reduce_fusion
  371.5 0.6 broadcast_in_dim.8
  372.1 5.5 %all-to-all-start.4 = ((bf16[16,1,2]{2,1,0:T(2,128)(2,1)}), bf16[16,1,2]{2,1,0:T(2,128)(2,1)S(1)}, u32[]{:S(2)}, u32[]{:S(2)}) async-start(bf16[16,1,2]{2,1,0:T(2,128)(2,1)} %broadcast_in_dim.8), calls=%async_computation.4 | async-start | bytes 16384 | tf_op jit(solution)/shard_map/all_to_all | solution.py:15
  377.6 7.3 %all-to-all-done.4 = bf16[16,1,2]{2,1,0:T(2,128)(2,1)S(1)} async-done(((bf16[16,1,2]{2,1,0:T(2,128)(2,1)}), bf16[16,1,2]{2,1,0:T(2,128)(2,1)S(1)}, u32[]{:S(2)}, u32[]{:S(2)}) %all-to-all-start.4) | async-done | bytes 96 | tf_op jit(solution)/shard_map/all_to_all | solution.py:15
  384.9 0.9 broadcast_in_dim.7
  385.8 3.5 all-to-all-start.3
  389.3 0.1 copy.21
  389.4 0.1 convert_reduce_fusion.2
  389.5 8.6 %all-to-all-done.3 = bf16[16,2,4096]{2,1,0:T(2,128)(2,1)S(1)} async-done(((bf16[16,2,4096]{2,1,0:T(2,128)(2,1)}), bf16[16,2,4096]{2,1,0:T(2,128)(2,1)S(1)}, u32[]{:S(2)}, u32[]{:S(2)}) %all-to-all-start.3) | async-done | bytes 262176 | tf_op jit(solution)/shard_map/all_to_all | solution.py:15
  398.1 0.2 convert_reduce_fusion.1
  398.4 0.7 add_divide_fusion
  399.1 46.0 %all-gather = bf16[32,2,4096]{2,1,0:T(2,128)(2,1)S(1)} all-gather(bf16[1,2,4096]{2,1,0:T(2,128)(2,1)S(1)} %get-tuple-element.3), channel_id=1, replica_groups=mesh['list'=32,'shard'=16] {'list'}, dimensions={0}, use_global_device_ids=true | all-gather | bytes 540672 | tf_op jit(solution)/shard_map/all_gather | solution.py:72
  445.0 0.2 reshape.51
  445.2 0.9 fusion.2
  (19 shorter events, 0.3 us)
Async XLA Ops:
  7.2 179.7 %all-gather.4.cloned.1.call-start = ((), (), s32[]{:S(2)}) async-start(), calls=%async_computation.5 | async-start | bytes 5988352 | tf_op jit(solution)/shard_map/all_gather | solution.py:24
  9.0 257.9 %all-gather.6.cloned.1.call-start = ((), (), s32[]{:S(2)}) async-start(), calls=%async_computation.6 | async-start | bytes 2994176 | tf_op jit(solution)/shard_map/all_gather | solution.py:65
  274.6 19.3 %copy-start.4 = (s32[8]{0:T(128)S(1)}, s32[8]{0:T(128)}, u32[]{:S(2)}) copy-start(s32[8]{0:T(128)} %param.15) | copy-start | bytes 100
  274.6 19.4 %copy-start.3 = (s32[8]{0:T(128)S(1)}, s32[8]{0:T(128)}, u32[]{:S(2)}) copy-start(s32[8]{0:T(128)} %param.14) | copy-start | bytes 100
  274.6 70.6 %copy-start = (bf16[8,4096]{1,0:T(8,128)(2,1)S(1)}, bf16[8,4096]{1,0:T(8,128)(2,1)}, u32[]{:S(2)}) copy-start(bf16[8,4096]{1,0:T(8,128)(2,1)} %param.8) | copy-start | bytes 196612
  274.6 70.8 %copy-start.2 = (f32[4096]{0:T(1024)S(1)}, f32[4096]{0:T(1024)}, u32[]{:S(2)}) copy-start(f32[4096]{0:T(1024)} %param.9) | copy-start | bytes 49156
  274.6 70.3 %all-to-all-start.1 = ((bf16[32,8,4096]{2,1,0:T(8,128)(2,1)}), bf16[32,8,4096]{2,1,0:T(8,128)(2,1)S(1)}, u32[]{:S(2)}, u32[]{:S(2)}) async-start(bf16[32,8,4096]{2,1,0:T(8,128)(2,1)} %fusion), calls=%async_computation.1 | async-start | bytes 4194304 | tf_op jit(solution)/shard_map/all_to_all | solution.py:38
  345.5 52.9 %copy-start.1 = (f32[2,4096]{1,0:T(2,128)S(1)}, f32[2,4096]{1,0:T(2,128)}, u32[]{:S(2)}) copy-start(f32[2,4096]{1,0:T(2,128)} %param.13) | copy-start | bytes 98308
  372.1 12.8 %all-to-all-start.4 = ((bf16[16,1,2]{2,1,0:T(2,128)(2,1)}), bf16[16,1,2]{2,1,0:T(2,128)(2,1)S(1)}, u32[]{:S(2)}, u32[]{:S(2)}) async-start(bf16[16,1,2]{2,1,0:T(2,128)(2,1)} %broadcast_in_dim.8), calls=%async_computation.4 | async-start | bytes 16384 | tf_op jit(solution)/shard_map/all_to_all | solution.py:15
  385.8 12.4 %all-to-all-start.3 = ((bf16[16,2,4096]{2,1,0:T(2,128)(2,1)}), bf16[16,2,4096]{2,1,0:T(2,128)(2,1)S(1)}, u32[]{:S(2)}, u32[]{:S(2)}) async-start(bf16[16,2,4096]{2,1,0:T(2,128)(2,1)} %broadcast_in_dim.7), calls=%async_computation.3 | async-start | bytes 524288 | tf_op jit(solution)/shard_map/all_to_all | solution.py:15
Sparse Core Ops, SparseCore 0:
  10.0 176.8 all-gather.3
  188.9 77.9 all-gather.5
where the time goes:
time: 453 us
  waiting for transfers between devices  239 us (53%)
  blocking collectives  151 us (33%)
  starting transfers between devices  28.4 us (6%)
  between operations  14.2 us (3%)
  matrix products  12.2 us (3%)
    all_gather x1, waiting for transfers between devices, in_one_piece(): filled, at, done = (lax.all_gather(both, axis, axis=dim, tiled=True), 0, [])  94.7 us
    all_to_all x1, blocking collectives, from_everyone(): return lax.all_to_all(copies, axis, split_axis=0, concat_axis=0, tiled=True)  81.3 us
    all_gather x1, waiting for transfers between devices, body(): lax.all_gather(down_weight, 'shard', axis=1, tiled=True)  77.1 us
    all_to_all x1, waiting for transfers between devices, sum_at_owner(): parts = lax.all_to_all(split_up(value, dim, peers), axis, 0, 0, tiled=True)  50.7 us
    all_gather x1, blocking collectives, body(): lax.all_gather(centroids.astype(jnp.bfloat16), 'list', axis=0, tiled=True)  46 us
    all_to_all x1, blocking collectives, sum_at_owner(): parts = lax.all_to_all(split_up(value, dim, peers), axis, 0, 0, tiled=True)  23.8 us
    all_to_all x1, starting transfers between devices, sum_at_owner(): parts = lax.all_to_all(split_up(value, dim, peers), axis, 0, 0, tiled=True)  19.3 us
    all_to_all x2, waiting for transfers between devices, from_everyone(): return lax.all_to_all(copies, axis, split_axis=0, concat_axis=0, tiled=True)  15.9 us
  transfers between devices with their start and end apart: 5, of which 5 were waited for; matrix products, arithmetic and copies ran while one was open for 1% of the time, Pallas kernels for 0%

commit v1 on v0

v1 whole, which is shorter than its diff:
```python
import jax
import jax.numpy as jnp
from jax import lax
from jax.sharding import Mesh, PartitionSpec as P

F32 = jnp.float32
BF16 = jnp.bfloat16
SWAP = [(0, 1), (1, 0)]
ROWS = ("yh", "x")
LIST = ("yh", "x", "c")
SHARD = ("z", "yl")


def swapped(value, axis):
    return lax.ppermute(value, axis, SWAP)


def to_everyone(value, axis):
    copies = jnp.broadcast_to(value, (lax.axis_size(axis), *value.shape))
    return lax.all_to_all(copies, axis, split_axis=0, concat_axis=0, tiled=True)


def by_class(value, mine):
    blocks = value.reshape(*value.shape[:-1], 8, 2, 256)
    even = blocks[..., 0, :].reshape(*value.shape[:-1], 2048)
    odd = blocks[..., 1, :].reshape(*value.shape[:-1], 2048)
    return jnp.where(mine == 0, even, odd), jnp.where(mine == 0, odd, even)


def interleaved(own, other, mine):
    even, odd = jnp.where(mine == 0, own, other), jnp.where(mine == 0, other, own)
    shape = own.shape[:-1]
    both = jnp.stack([even.reshape(*shape, 8, 256), odd.reshape(*shape, 8, 256)], axis=-2)
    return both.reshape(*shape, 4096)


def gate_up(rows, weights):
    return jnp.einsum("rzk,zhk->rh", rows, weights, preferred_element_type=F32)


def down(hidden, weights):
    return jnp.einsum("rh,zhk->rzk", hidden, weights, preferred_element_type=F32)


def body(features, norm_gain, gate_weight, up_weight, down_weight, centroids, list_ids, live):
    yl = lax.axis_index("yl")
    first = jnp.concatenate([gate_weight.T, up_weight.T], axis=0)
    first = lax.all_gather(first, "z", axis=0, tiled=False)
    second = lax.all_gather(down_weight, "z", axis=0, tiled=False)

    code = jnp.where(live > 0, list_ids, -1).astype(BF16)
    own_x, away_x = by_class(features, yl)
    code_block = jnp.broadcast_to(code[:, None], (8, 128))
    received = swapped(jnp.concatenate([away_x, code_block], axis=1), "yl")
    x = jnp.concatenate([own_x, received[:, :2048]], axis=0)
    codes = jnp.concatenate([code, received[:, 2048]], axis=0)
    table, _ = by_class(centroids.astype(BF16), yl)
    sent = jnp.concatenate([x, table.reshape(16, 256)], axis=1)
    mine = to_everyone(sent, ROWS)
    theirs = swapped(mine, "c")
    both = jnp.stack([mine, theirs])
    rows = both[..., :2048].reshape(2, 16, 2, 8, 8, 256)
    kept = rows[:, :, 0].reshape(256, 8, 256)
    away = rows[:, :, 1].reshape(256, 8, 256)
    core = lax.axis_index("c")
    lists = both[..., 2048:].reshape(2, 16, 2, 2048)
    lists = jnp.where(core == 0, lists, lists[::-1])
    lists = lists.transpose(1, 0, 2, 3).reshape(64, 2048)

    away_part = gate_up(away, first).astype(BF16)
    away_part = swapped(away_part, "yl")
    whole = gate_up(kept, first) + away_part.astype(F32)
    hidden = (jax.nn.silu(whole[:, :344]) * whole[:, 344:]).astype(BF16)
    other_hidden = swapped(hidden, "yl")
    hidden = jnp.stack([hidden.reshape(2, 128, 344), other_hidden.reshape(2, 128, 344)], axis=1)
    hidden = hidden.reshape(2, 256, 344)
    to_core = down(hidden[1], second).astype(BF16)
    from_core = swapped(to_core, "c")
    terms = (down(hidden[0], second) + from_core.astype(F32)).astype(BF16)
    terms = terms.reshape(2, 16, 8, 2048).transpose(1, 0, 2, 3).reshape(16, 16, 2048)
    terms = lax.all_to_all(terms, ROWS, 0, 0, tiled=True)
    stream = x.astype(F32) + jnp.sum(terms.astype(F32), axis=0)

    square = jnp.sum(stream * stream, axis=1, keepdims=True)
    other_square = swapped(jnp.broadcast_to(square, (16, 128)), "yl")[:, :1]
    other_square = jnp.concatenate([other_square[8:], other_square[:8]], axis=0)
    scale = lax.rsqrt((square + other_square) / 4096.0 + 1e-05)
    gain, _ = by_class(norm_gain, yl)
    embedding = (stream * scale * gain).astype(BF16)

    member = (codes[:, None] == jnp.arange(64, dtype=F32)[None, :].astype(BF16)).astype(BF16)
    alive = (codes >= 0).astype(F32)
    coarse = jnp.dot(member, lists, preferred_element_type=F32)
    residual = (alive[:, None] * (embedding.astype(F32) - coarse)).astype(BF16)
    residuals = interleaved(residual[:8], swapped(residual[8:], "yl"), yl)

    sums = jnp.dot(member.T, embedding, preferred_element_type=F32).astype(BF16)
    counts = jnp.sum(member.astype(F32), axis=0).astype(BF16)
    sums = jnp.concatenate([sums, jnp.broadcast_to(counts[:, None], (64, 128))], axis=1)
    sums = lax.all_to_all(sums.reshape(32, 2, 2176), LIST, 0, 0, tiled=True)
    sums = jnp.sum(sums.astype(F32), axis=0)
    total = to_everyone(sums, SHARD).reshape(8, 2, 2, 2176).sum(axis=0)
    even, odd = total[0], total[1]
    total_counts = even[:, 2048:2049]
    total_sums = jnp.stack(
        [even[:, :2048].reshape(2, 8, 256), odd[:, :2048].reshape(2, 8, 256)], axis=2
    ).reshape(2, 4096)
    refreshed = (centroids + total_sums) / (1.0 + total_counts)
    return residuals, refreshed


def solution(mesh):
    fine = Mesh(mesh.devices.reshape(4, 4, 2, 8, 2), ("yh", "x", "c", "z", "yl"))
    in_specs = (
        P((*LIST, *SHARD), None),
        P(),
        P(SHARD, LIST),
        P(SHARD, LIST),
        P(LIST, SHARD),
        P(LIST, None),
        P((*LIST, *SHARD)),
        P((*LIST, *SHARD)),
    )
    out_specs = (P((*LIST, *SHARD), None), P(LIST, None))
    return jax.shard_map(body, mesh=fine, in_specs=in_specs, out_specs=out_specs, check_vma=False)
```

time: 453 us -> 209 us (0.46)
  waiting for transfers between devices: 239 us -> 80.5 us
  blocking collectives: 151 us -> 40.1 us
  starting transfers between devices: 28.4 us -> 44.9 us
  local copies, waits for them, and re-layouts: 3.5 us -> 9.59 us
    all_gather x2, waiting for transfers between devices: 172 us -> 11.6 us  [the longest x1 11.5 us: body(): second = lax.all_gather(down_weight, 'z', axis=0, tiled=False)]
    all_to_all x2 -> x1, blocking collectives: 105 us -> 40.1 us  [to_everyone(): return lax.all_to_all(copies, axis, split_axis=0, concat_axis=0, tiled=True)]
    all_gather x1 -> x0, blocking collectives: 46 us -> none  [body(): lax.all_gather(centroids.astype(jnp.bfloat16), 'list', axis=0, tiled=True)]
    ppermute x0 -> x7, starting transfers between devices: none -> 23.5 us  [swapped(): return lax.ppermute(value, axis, SWAP)]
    ppermute x0 -> x7, waiting for transfers between devices: none -> 21.7 us  [swapped(): return lax.ppermute(value, axis, SWAP)]
    all_to_all x3, waiting for transfers between devices: 66.6 us -> 47.2 us  [the longest x1 26.6 us: body(): terms = lax.all_to_all(terms, ROWS, 0, 0, tiled=True)]
    all_to_all x3, starting transfers between devices: 28.3 us -> 21.3 us  [the longest x1 9.06 us: body(): terms = lax.all_to_all(terms, ROWS, 0, 0, tiled=True)]
    dot_general x4 -> x6, matrix products: 12.2 us -> 9.5 us  [the longest x2 5.15 us: down(): jnp.einsum('rh,zhk->rzk', hidden, weights, preferred_element_type=F32)]
  transfers between devices with their start and end apart: 5 -> 12, of which waited for: 5 -> 10; matrix products, arithmetic and copies ran while one was open for 1% -> 6% of each run, Pallas kernels for 0% -> 0%
where the time goes in v1:
time: 209 us; the launch traced here: 208 us
  waiting for transfers between devices  80.5 us (39%)
  starting transfers between devices  44.9 us (21%)
  blocking collectives  40.1 us (19%)
  between operations  14.6 us (7%)
  local copies, waits for them, and re-layouts  9.59 us (5%)
  matrix products  9.5 us (5%)
  other arithmetic  8.38 us (4%)
    all_to_all x1, blocking collectives, to_everyone(): return lax.all_to_all(copies, axis, split_axis=0, concat_axis=0, tiled=True)  40.1 us
    all_to_all x1, waiting for transfers between devices, body(): terms = lax.all_to_all(terms, ROWS, 0, 0, tiled=True)  26.6 us
    ppermute x7, starting transfers between devices, swapped(): return lax.ppermute(value, axis, SWAP)  23.5 us
    ppermute x7, waiting for transfers between devices, swapped(): return lax.ppermute(value, axis, SWAP)  21.7 us
    all_gather x1, waiting for transfers between devices, body(): second = lax.all_gather(down_weight, 'z', axis=0, tiled=False)  11.5 us
    all_to_all x1, waiting for transfers between devices, body(): sums = lax.all_to_all(sums.reshape(32, 2, 2176), LIST, 0, 0, tiled=True)  10.6 us
    all_to_all x1, waiting for transfers between devices, to_everyone(): return lax.all_to_all(copies, axis, split_axis=0, concat_axis=0, tiled=True)  10 us
    all_to_all x1, starting transfers between devices, body(): terms = lax.all_to_all(terms, ROWS, 0, 0, tiled=True)  9.06 us
  transfers between devices with their start and end apart: 12, of which 10 were waited for; matrix products, arithmetic and copies ran while one was open for 6% of the time, Pallas kernels for 0%

profile of v1, /device:TPU:1, one launch (start us, length us, event | category | flops | bytes accessed | tf_op | source)
XLA Modules:
  0.0 207.6 jit_solution(13184485440422536307)
XLA Ops:
  7.2 1.8 pad_maximum_fusion
  9.7 0.8 broadcast_select_fusion.1
  10.6 4.0 %collective-permute-start = (bf16[8,2176]{1,0:T(8,128)(2,1)S(1)}, bf16[8,2176]{1,0:T(8,128)(2,1)S(1)}, u32[]{:S(2)}, u32[]{:S(2)}) collective-permute-start(bf16[8,2176]{1,0:T(8,128)(2,1)S(1)} %pad_maximum_fusion.6), channel_id=1, source_target_pairs={{0,1},{1,0},{2,3},{3,2},{4,5},{5,4},{6,7},{7,6},{8,9},{9,8},{10,11... | collective-permute-start | bytes 104456 | tf_op jit(solution)/shard_map/ppermute | solution.py:15
  14.6 0.8 convert_element_type.68
  16.7 40.1 %all_to_all.20 = bf16[16,16,2304]{2,1,0:T(8,128)(2,1)S(1)} all-to-all(bf16[16,16,2304]{2,1,0:T(8,128)(2,1)S(1)} %broadcast_in_dim.16), channel_id=1, replica_groups=mesh['yh'=4,'x'=4,'c'=2,'z'=8,'yl'=2] {'yh','x'}, dimensions={0} | all-to-all | bytes 2359296 | tf_op jit(solution)/shard_map/all_to_all | solution.py:20
  56.7 4.6 %collective-permute-start.1 = (bf16[16,16,2304]{2,1,0:T(8,128)(2,1)S(1)}, bf16[16,16,2304]{2,1,0:T(8,128)(2,1)S(1)}, u32[]{:S(2)}, u32[]{:S(2)}) collective-permute-start(bf16[16,16,2304]{2,1,0:T(8,128)(2,1)S(1)} %all_to_all.20), channel_id=1, source_target_pairs={{0,16},{16,0},{1,17},{17,1},{2,18},{18,2},{3,19},{19,3},{4,20},{20... | collective-permute-start | bytes 3538952 | tf_op jit(solution)/shard_map/ppermute | solution.py:15
  61.3 2.4 %collective-permute-done.1 = bf16[16,16,2304]{2,1,0:T(8,128)(2,1)S(1)} collective-permute-done((bf16[16,16,2304]{2,1,0:T(8,128)(2,1)S(1)}, bf16[16,16,2304]{2,1,0:T(8,128)(2,1)S(1)}, u32[]{:S(2)}, u32[]{:S(2)}) %collective-permute-start.1) | collective-permute-done | bytes 1179680 | tf_op jit(solution)/shard_map/ppermute | solution.py:15
  63.9 0.8 copy-done.1
  65.9 2.9 %fusion.3 = bf16[256,688]{0,1:T(8,128)(2,1)S(1)} fusion(bf16[256,8,256]{2,0,1:T(8,128)(2,1)S(1)} %bitcast.96, bf16[8,688,256]{2,1,0:T(8,128)(2,1)} %bitcast.110), kind=kOutput, calls=%fused_computation.12 | convolution fusion | flops 721596416 | bytes 4218880 | tf_op jit(solution)/shard_map/rzk,zhk->rh/dot_general | solution.py:38
  68.8 1.9 collective-permute-start.2
  70.9 9.3 %collective-permute-done.2 = bf16[256,688]{0,1:T(8,128)(2,1)S(1)} collective-permute-done((bf16[256,688]{0,1:T(8,128)(2,1)S(1)}, bf16[256,688]{0,1:T(8,128)(2,1)S(1)}, u32[]{:S(2)}, u32[]{:S(2)}) %collective-permute-start.2) | collective-permute-done | bytes 352288 | tf_op jit(solution)/shard_map/ppermute | solution.py:15
  80.2 0.9 convert_add_fusion
  81.2 2.1 %collective-permute-start.3 = (bf16[256,344]{0,1:T(8,128)(2,1)S(1)}, bf16[256,344]{0,1:T(8,128)(2,1)S(1)}, u32[]{:S(2)}, u32[]{:S(2)}) collective-permute-start(bf16[256,344]{0,1:T(8,128)(2,1)S(1)} %fusion.4), channel_id=1, source_target_pairs={{0,1},{1,0},{2,3},{3,2},{4,5},{5,4},{6,7},{7,6},{8,9},{9,8},{10,11... | collective-permute-start | bytes 528392 | tf_op jit(solution)/shard_map/ppermute | solution.py:15
  83.5 4.5 %collective-permute-done.3 = bf16[256,344]{0,1:T(8,128)(2,1)S(1)} collective-permute-done((bf16[256,344]{0,1:T(8,128)(2,1)S(1)}, bf16[256,344]{0,1:T(8,128)(2,1)S(1)}, u32[]{:S(2)}, u32[]{:S(2)}) %collective-permute-start.3) | collective-permute-done | bytes 176160 | tf_op jit(solution)/shard_map/ppermute | solution.py:15
  89.0 11.5 %all-gather.7.cloned.1.call-done = bf16[2752,256]{1,0:T(8,128)(2,1)} async-done(((bf16[344,256]{1,0:T(8,128)(2,1)}), bf16[2752,256]{1,0:T(8,128)(2,1)}) %all-gather.7.cloned.1.call-update) | async-done | bytes 1409040 | tf_op jit(solution)/shard_map/all_gather | solution.py:49
  100.6 3.2 %convolution_convert_fusion.1 = bf16[256,8,256]{2,0,1:T(8,128)(2,1)} fusion(bf16[256,344,1]{0,1,2:T(8,128)(2,1)S(1)} %reshape.133, bf16[8,344,256]{2,1,0:T(8,128)(2,1)} %bitcast.90), kind=kOutput, calls=%fused_computation.9 | convolution fusion | flops 361234432 | bytes 2633728 | tf_op jit(solution)/shard_map/rh,zhk->rzk/dot_general | solution.py:42
  103.8 7.1 %collective-permute-start.4 = (bf16[256,8,256]{2,0,1:T(8,128)(2,1)}, bf16[256,8,256]{2,0,1:T(8,128)(2,1)}, u32[]{:S(2)}, u32[]{:S(2)}) collective-permute-start(bf16[256,8,256]{2,0,1:T(8,128)(2,1)} %convolution_convert_fusion.1), channel_id=1, source_target_pairs={{0,16},{16,0},{1,17},{17,1},{2,18},{18,2},{3,19},{19,3},{4,20},{20... | collective-permute-start | bytes 3145736 | tf_op jit(solution)/shard_map/ppermute | solution.py:15
  111.2 2.3 %collective-permute-done.4 = bf16[256,8,256]{2,0,1:T(8,128)(2,1)} collective-permute-done((bf16[256,8,256]{2,0,1:T(8,128)(2,1)}, bf16[256,8,256]{2,0,1:T(8,128)(2,1)}, u32[]{:S(2)}, u32[]{:S(2)}) %collective-permute-start.4) | collective-permute-done | bytes 1048608 | tf_op jit(solution)/shard_map/ppermute | solution.py:15
  113.5 2.0 add_convert_fusion
  116.6 1.0 copy_bitcast_fusion
  117.7 9.1 %all-to-all-start.1 = ((bf16[16,16,2048]{2,1,0:T(8,128)(2,1)}), bf16[16,16,2048]{2,1,0:T(8,128)(2,1)S(1)}, u32[]{:S(2)}, u32[]{:S(2)}) async-start(bf16[16,16,2048]{2,1,0:T(8,128)(2,1)} %copy_bitcast_fusion), calls=%async_computation.1 | async-start | bytes 2097152 | tf_op jit(solution)/shard_map/all_to_all | solution.py:81
  128.2 26.6 %all-to-all-done.1 = bf16[16,16,2048]{2,1,0:T(8,128)(2,1)S(1)} async-done(((bf16[16,16,2048]{2,1,0:T(8,128)(2,1)}), bf16[16,16,2048]{2,1,0:T(8,128)(2,1)S(1)}, u32[]{:S(2)}, u32[]{:S(2)}) %all-to-all-start.1) | async-done | bytes 1048608 | tf_op jit(solution)/shard_map/all_to_all | solution.py:81
  154.9 1.0 multiply_reduce_fusion
  155.9 1.9 collective-permute-start.5
  158.2 2.7 %collective-permute-done.5 = f32[16,128]{0,1:T(8,128)S(1)} collective-permute-done((f32[16,128]{0,1:T(8,128)S(1)}, f32[16,128]{0,1:T(8,128)S(1)}, u32[]{:S(2)}, u32[]{:S(2)}) %collective-permute-start.5) | collective-permute-done | bytes 8224 | tf_op jit(solution)/shard_map/ppermute | solution.py:15
  161.6 0.8 reshape.125
  162.4 8.4 %all-to-all-start.2 = ((bf16[32,2,2176]{2,1,0:T(2,128)(2,1)}), bf16[32,2,2176]{2,1,0:T(2,128)(2,1)S(1)}, u32[]{:S(2)}, u32[]{:S(2)}) async-start(bf16[32,2,2176]{2,1,0:T(2,128)(2,1)} %reshape.125), calls=%async_computation.2 | async-start | bytes 557056 | tf_op jit(solution)/shard_map/all_to_all | solution.py:100
  171.5 1.9 collective-permute-start.6
  173.4 10.6 %all-to-all-done.2 = bf16[32,2,2176]{2,1,0:T(2,128)(2,1)S(1)} async-done(((bf16[32,2,2176]{2,1,0:T(2,128)(2,1)}), bf16[32,2,2176]{2,1,0:T(2,128)(2,1)S(1)}, u32[]{:S(2)}, u32[]{:S(2)}) %all-to-all-start.2) | async-done | bytes 278560 | tf_op jit(solution)/shard_map/all_to_all | solution.py:100
  184.3 0.8 broadcast_in_dim.19
  185.0 3.9 %all-to-all-start.3 = ((f32[16,2,2176]{2,1,0:T(2,128)}), f32[16,2,2176]{2,1,0:T(2,128)S(1)}, u32[]{:S(2)}, u32[]{:S(2)}) async-start(f32[16,2,2176]{2,1,0:T(2,128)} %broadcast_in_dim.19), calls=%async_computation.3 | async-start | bytes 557056 | tf_op jit(solution)/shard_map/all_to_all | solution.py:20
  189.6 10.0 %all-to-all-done.3 = f32[16,2,2176]{2,1,0:T(2,128)S(1)} async-done(((f32[16,2,2176]{2,1,0:T(2,128)}), f32[16,2,2176]{2,1,0:T(2,128)S(1)}, u32[]{:S(2)}, u32[]{:S(2)}) %all-to-all-start.3) | async-done | bytes 278560 | tf_op jit(solution)/shard_map/all_to_all | solution.py:20
  (91 shorter events, 11.4 us)
Async XLA Ops:
  7.2 58.7 %all-gather.5.cloned.1.call-start = ((), (), s32[]{:S(2)}) async-start(), calls=%async_computation.4 | async-start | bytes 3170304 | tf_op jit(solution)/shard_map/all_gather | solution.py:48
  9.0 91.6 %all-gather.7.cloned.1.call-start = ((), (), s32[]{:S(2)}) async-start(), calls=%async_computation.5 | async-start | bytes 1585152 | tf_op jit(solution)/shard_map/all_gather | solution.py:49
  10.5 6.0 %copy-start.5 = (bf16[8,8,1,256]{3,0,1,2:T(8,128)(2,1)}, bf16[8,8,1,256]{3,0,1,2:T(8,128)(2,1)S(1)}, u32[]{:S(2)}) copy-start(bf16[8,8,1,256]{3,0,1,2:T(8,128)(2,1)S(1)} %get-tuple-element.12) | copy-start | bytes 98308
  10.6 5.3 %collective-permute-start = (bf16[8,2176]{1,0:T(8,128)(2,1)S(1)}, bf16[8,2176]{1,0:T(8,128)(2,1)S(1)}, u32[]{:S(2)}, u32[]{:S(2)}) collective-permute-start(bf16[8,2176]{1,0:T(8,128)(2,1)S(1)} %pad_maximum_fusion.6), channel_id=1, source_target_pairs={{0,1},{1,0},{2,3},{3,2},{4,5},{5,4},{6,7},{7,6},{8,9},{9,8},{10,11... | collective-permute-start | bytes 104456 | tf_op jit(solution)/shard_map/ppermute | solution.py:15
  15.9 0.6 copy-start.3
  56.7 7.0 %collective-permute-start.1 = (bf16[16,16,2304]{2,1,0:T(8,128)(2,1)S(1)}, bf16[16,16,2304]{2,1,0:T(8,128)(2,1)S(1)}, u32[]{:S(2)}, u32[]{:S(2)}) collective-permute-start(bf16[16,16,2304]{2,1,0:T(8,128)(2,1)S(1)} %all_to_all.20), channel_id=1, source_target_pairs={{0,16},{16,0},{1,17},{17,1},{2,18},{18,2},{3,19},{19,3},{4,20},{20... | collective-permute-start | bytes 3538952 | tf_op jit(solution)/shard_map/ppermute | solution.py:15
  63.7 1.0 copy-start.1
  65.9 14.3 %copy-start.11 = (bf16[5504,256]{1,0:T(8,128)(2,1)S(1)}, bf16[5504,256]{1,0:T(8,128)(2,1)}, u32[]{:S(2)}) copy-start(bf16[5504,256]{1,0:T(8,128)(2,1)} %all-gather.5.cloned.1.call-done) | copy-start | bytes 8454148
  68.8 11.4 %collective-permute-start.2 = (bf16[256,688]{0,1:T(8,128)(2,1)S(1)}, bf16[256,688]{0,1:T(8,128)(2,1)S(1)}, u32[]{:S(2)}, u32[]{:S(2)}) collective-permute-start(bf16[256,688]{0,1:T(8,128)(2,1)S(1)} %fusion.3), channel_id=1, source_target_pairs={{0,1},{1,0},{2,3},{3,2},{4,5},{5,4},{6,7},{7,6},{8,9},{9,8},{10,11... | collective-permute-start | bytes 1056776 | tf_op jit(solution)/shard_map/ppermute | solution.py:15
  81.2 6.8 %collective-permute-start.3 = (bf16[256,344]{0,1:T(8,128)(2,1)S(1)}, bf16[256,344]{0,1:T(8,128)(2,1)S(1)}, u32[]{:S(2)}, u32[]{:S(2)}) collective-permute-start(bf16[256,344]{0,1:T(8,128)(2,1)S(1)} %fusion.4), channel_id=1, source_target_pairs={{0,1},{1,0},{2,3},{3,2},{4,5},{5,4},{6,7},{7,6},{8,9},{9,8},{10,11... | collective-permute-start | bytes 528392 | tf_op jit(solution)/shard_map/ppermute | solution.py:15
  100.6 12.9 %copy-start = (bf16[2752,256]{1,0:T(8,128)(2,1)S(1)}, bf16[2752,256]{1,0:T(8,128)(2,1)}, u32[]{:S(2)}) copy-start(bf16[2752,256]{1,0:T(8,128)(2,1)} %all-gather.7.cloned.1.call-done) | copy-start | bytes 4227076
  103.8 9.7 %collective-permute-start.4 = (bf16[256,8,256]{2,0,1:T(8,128)(2,1)}, bf16[256,8,256]{2,0,1:T(8,128)(2,1)}, u32[]{:S(2)}, u32[]{:S(2)}) collective-permute-start(bf16[256,8,256]{2,0,1:T(8,128)(2,1)} %convolution_convert_fusion.1), channel_id=1, source_target_pairs={{0,16},{16,0},{1,17},{17,1},{2,18},{18,2},{3,19},{19,3},{4,20},{20... | collective-permute-start | bytes 3145736 | tf_op jit(solution)/shard_map/ppermute | solution.py:15
  116.6 10.1 %copy-start.8 = (f32[4096]{0:T(1024)S(1)}, f32[4096]{0:T(1024)}, u32[]{:S(2)}) copy-start(f32[4096]{0:T(1024)} %param.9) | copy-start | bytes 49156
  117.7 40.2 %copy-start.2 = (bf16[16,16,2304]{2,1,0:T(8,128)(2,1)S(1)}, bf16[16,16,2304]{2,1,0:T(8,128)(2,1)}, u32[]{:S(2)}) copy-start(bf16[16,16,2304]{2,1,0:T(8,128)(2,1)} %copy-done.1) | copy-start | bytes 3538948
  117.7 37.1 %all-to-all-start.1 = ((bf16[16,16,2048]{2,1,0:T(8,128)(2,1)}), bf16[16,16,2048]{2,1,0:T(8,128)(2,1)S(1)}, u32[]{:S(2)}, u32[]{:S(2)}) async-start(bf16[16,16,2048]{2,1,0:T(8,128)(2,1)} %copy_bitcast_fusion), calls=%async_computation.1 | async-start | bytes 2097152 | tf_op jit(solution)/shard_map/all_to_all | solution.py:81
  154.9 6.2 %copy-start.4 = (bf16[8,2048]{1,0:T(8,128)(2,1)S(1)}, bf16[8,2048]{1,0:T(8,128)(2,1)}, u32[]{:S(2)}) copy-start(bf16[8,2048]{1,0:T(8,128)(2,1)} %copy-done.3) | copy-start | bytes 98308
  154.9 6.2 %copy-start.6 = (bf16[8,8,1,256]{3,0,1,2:T(8,128)(2,1)S(1)}, bf16[8,8,1,256]{3,0,1,2:T(8,128)(2,1)}, u32[]{:S(2)}) copy-start(bf16[8,8,1,256]{3,0,1,2:T(8,128)(2,1)} %copy-done.5) | copy-start | bytes 98308
  155.9 5.6 %copy-start.10 = (bf16[64]{0:T(256)(128)(2,1)S(1)}, bf16[64]{0:T(256)(128)(2,1)}, u32[]{:S(2)}) copy-start(bf16[64]{0:T(256)(128)(2,1)} %fusion.9) | copy-start | bytes 388
  155.9 5.0 %collective-permute-start.5 = (f32[16,128]{0,1:T(8,128)S(1)}, f32[16,128]{0,1:T(8,128)S(1)}, u32[]{:S(2)}, u32[]{:S(2)}) collective-permute-start(f32[16,128]{0,1:T(8,128)S(1)} %broadcast_in_dim.17), channel_id=1, source_target_pairs={{0,1},{1,0},{2,3},{3,2},{4,5},{5,4},{6,7},{7,6},{8,9},{9,8},{10,11... | collective-permute-start | bytes 24584 | tf_op jit(solution)/shard_map/ppermute | solution.py:15
  157.9 13.3 %copy-start.9 = (f32[16]{0:T(128)S(1)}, f32[16]{0:T(128)}, u32[]{:S(2)}) copy-start(f32[16]{0:T(128)} %get-tuple-element.2) | copy-start | bytes 196
  162.4 37.6 %copy-start.7 = (f32[2,4096]{1,0:T(2,128)S(1)}, f32[2,4096]{1,0:T(2,128)}, u32[]{:S(2)}) copy-start(f32[2,4096]{1,0:T(2,128)} %param.13) | copy-start | bytes 98308
  162.4 21.6 %all-to-all-start.2 = ((bf16[32,2,2176]{2,1,0:T(2,128)(2,1)}), bf16[32,2,2176]{2,1,0:T(2,128)(2,1)S(1)}, u32[]{:S(2)}, u32[]{:S(2)}) async-start(bf16[32,2,2176]{2,1,0:T(2,128)(2,1)} %reshape.125), calls=%async_computation.2 | async-start | bytes 557056 | tf_op jit(solution)/shard_map/all_to_all | solution.py:100
  171.5 17.5 %collective-permute-start.6 = (bf16[8,2048]{1,0:T(8,128)(2,1)S(1)}, bf16[8,2048]{1,0:T(8,128)(2,1)S(1)}, u32[]{:S(2)}, u32[]{:S(2)}) collective-permute-start(bf16[8,2048]{1,0:T(8,128)(2,1)S(1)} %slice.124), channel_id=1, source_target_pairs={{0,1},{1,0},{2,3},{3,2},{4,5},{5,4},{6,7},{7,6},{8,9},{9,8},{10,11... | collective-permute-start | bytes 98312 | tf_op jit(solution)/shard_map/ppermute | solution.py:15
  185.0 14.6 %all-to-all-start.3 = ((f32[16,2,2176]{2,1,0:T(2,128)}), f32[16,2,2176]{2,1,0:T(2,128)S(1)}, u32[]{:S(2)}, u32[]{:S(2)}) async-start(f32[16,2,2176]{2,1,0:T(2,128)} %broadcast_in_dim.19), calls=%async_computation.3 | async-start | bytes 557056 | tf_op jit(solution)/shard_map/all_to_all | solution.py:20
Sparse Core Ops, SparseCore 0:
  10.1 49.6 all-gather.4
  61.8 38.7 all-gather.6

commit v2 on v1

v2 whole, which is shorter than its diff:
```python
import jax
import jax.numpy as jnp
from jax import lax
from jax.sharding import Mesh, PartitionSpec as P

F32 = jnp.float32
BF16 = jnp.bfloat16
SWAP = [(0, 1), (1, 0)]
ROWS = ("x", "yh")
LIST = ("yh", "x", "c")
SHARD = ("z", "yl")


def swapped(value, axis):
    return lax.ppermute(value, axis, SWAP)


def to_everyone(value, axis):
    copies = jnp.broadcast_to(value, (lax.axis_size(axis), *value.shape))
    return lax.all_to_all(copies, axis, split_axis=0, concat_axis=0, tiled=True)


def by_class(value, mine):
    blocks = value.reshape(*value.shape[:-1], 8, 2, 256)
    even = blocks[..., 0, :].reshape(*value.shape[:-1], 2048)
    odd = blocks[..., 1, :].reshape(*value.shape[:-1], 2048)
    return jnp.where(mine == 0, even, odd), jnp.where(mine == 0, odd, even)


def interleaved(own, other, mine):
    even, odd = jnp.where(mine == 0, own, other), jnp.where(mine == 0, other, own)
    shape = own.shape[:-1]
    both = jnp.stack([even.reshape(*shape, 8, 256), odd.reshape(*shape, 8, 256)], axis=-2)
    return both.reshape(*shape, 4096)


def gate_up(rows, weights):
    return jnp.einsum("rzk,zhk->rh", rows, weights, preferred_element_type=F32)


def down(hidden, weights):
    return jnp.einsum("rh,zhk->zrk", hidden, weights, preferred_element_type=F32)


def one_hot(codes):
    return (codes[:, None] == jnp.arange(64, dtype=F32)[None, :].astype(BF16)).astype(BF16)


def body(features, norm_gain, gate_weight, up_weight, down_weight, centroids, list_ids, live):
    yl = lax.axis_index("yl")
    weights = jnp.concatenate([gate_weight.T, up_weight.T, down_weight], axis=0)
    weights = lax.all_gather(weights, "z", axis=0, tiled=False)
    first, second = weights[:, :688], weights[:, 688:]

    code = jnp.where(live > 0, list_ids, -1).astype(BF16)
    code_block = jnp.broadcast_to(code[:, None], (8, 128))
    own_x, away_x = by_class(features, yl)
    received = swapped(jnp.concatenate([away_x, code_block], axis=1), "yl")
    x = jnp.concatenate([own_x, received[:, :2048]], axis=0)
    other_code = received[:, 2048]
    table, _ = by_class(centroids.astype(BF16), yl)
    sent = jnp.concatenate([x, table.reshape(16, 256)], axis=1)
    mine = to_everyone(sent, ROWS)
    theirs = swapped(mine, "c")
    both = jnp.stack([mine, theirs])
    rows = both[..., :2048].reshape(2, 16, 2, 8, 8, 256)
    kept = rows[:, :, 0].reshape(256, 8, 256)
    away = rows[:, :, 1].reshape(256, 8, 256)
    core = lax.axis_index("c")
    lists = both[..., 2048:].reshape(2, 4, 4, 2, 2048)
    lists = jnp.where(core == 0, lists, lists[::-1])
    lists = lists.transpose(2, 1, 0, 3, 4).reshape(64, 2048)
    picked = jnp.dot(one_hot(code), lists, preferred_element_type=F32).astype(BF16)
    other_picked = jnp.dot(one_hot(other_code), lists, preferred_element_type=F32).astype(BF16)
    coarse = interleaved(picked, swapped(other_picked, "yl"), yl)

    away_part = gate_up(away, first).astype(BF16)
    away_part = swapped(away_part, "yl")
    whole = gate_up(kept, first) + away_part.astype(F32)
    hidden = (jax.nn.silu(whole[:, :344]) * whole[:, 344:]).astype(BF16)
    other_hidden = swapped(hidden, "yl")
    hidden = jnp.stack([hidden.reshape(2, 4, 32, 344), other_hidden.reshape(2, 4, 32, 344)], axis=2)
    hidden = hidden.reshape(2, 256, 344)
    to_core = down(hidden[1], second).astype(BF16)
    from_core = swapped(to_core, "c")
    terms = (down(hidden[0], second) + from_core.astype(F32)).astype(BF16)
    terms = terms.reshape(8, 4, 64, 256).transpose(1, 0, 2, 3)
    terms = lax.all_to_all(terms, "x", 0, 0, tiled=True)
    terms = jnp.sum(terms.astype(F32), axis=0).astype(BF16)
    terms = terms.reshape(8, 2, 4, 8, 256).transpose(2, 1, 0, 3, 4)
    terms = jnp.where(yl == 0, terms, terms[:, ::-1]).reshape(8, 8, 8, 256)
    terms = lax.all_to_all(terms, ("yh", "yl"), 0, 0, tiled=True)
    terms = jnp.sum(terms.reshape(4, 2, 8, 8, 256).astype(F32), axis=0)
    mixed = terms.transpose(2, 1, 0, 3).reshape(8, 4096)

    stream = features.astype(F32) + mixed
    scale = lax.rsqrt(jnp.mean(stream * stream, axis=1, keepdims=True) + 1e-05)
    embedding = (stream * scale * norm_gain).astype(BF16)
    alive = (live > 0).astype(F32)[:, None]
    residuals = (alive * (embedding.astype(F32) - coarse.astype(F32))).astype(BF16)

    blocks = embedding.reshape(8, 16, 256).transpose(1, 0, 2)
    blocks = jnp.concatenate([blocks, jnp.broadcast_to(code_block, (16, 8, 128))], axis=2)
    blocks = lax.all_to_all(blocks, SHARD, 0, 0, tiled=True).reshape(128, 384)
    member = one_hot(blocks[:, 256])
    sums = jnp.dot(member.T, blocks[:, :256], preferred_element_type=F32).astype(BF16)
    counts = jnp.sum(member.astype(F32), axis=0).astype(BF16)
    sums = jnp.concatenate([sums, jnp.broadcast_to(counts[:, None], (64, 128))], axis=1)
    sums = lax.all_to_all(sums.reshape(32, 2, 384), LIST, 0, 0, tiled=True)
    sums = jnp.sum(sums.astype(F32), axis=0)
    total = to_everyone(sums[:, :256], SHARD).transpose(1, 0, 2).reshape(2, 4096)
    refreshed = (centroids + total) / (1.0 + sums[:, 256:257])
    return residuals, refreshed


def solution(mesh):
    fine = Mesh(mesh.devices.reshape(4, 4, 2, 8, 2), ("yh", "x", "c", "z", "yl"))
    in_specs = (
        P((*LIST, *SHARD), None),
        P(),
        P(SHARD, LIST),
        P(SHARD, LIST),
        P(LIST, SHARD),
        P(LIST, None),
        P((*LIST, *SHARD)),
        P((*LIST, *SHARD)),
    )
    out_specs = (P((*LIST, *SHARD), None), P(LIST, None))
    return jax.shard_map(body, mesh=fine, in_specs=in_specs, out_specs=out_specs, check_vma=False)
```

time: 209 us -> 196 us (0.938)
  waiting for transfers between devices: 80.5 us -> 51.2 us
  blocking collectives: 40.1 us -> 69 us
  starting transfers between devices: 44.9 us -> 36.5 us
  local copies, waits for them, and re-layouts: 9.59 us -> 6.24 us
    all_to_all x0 -> x2, blocking collectives: none -> 28.6 us  [the longest x1 17.1 us: body(): sums = lax.all_to_all(sums.reshape(32, 2, 384), LIST, 0, 0, tiled=True)]
    all_to_all x2, waiting for transfers between devices: 37.2 us -> 20 us  [the longest x1 10.4 us: body(): terms = lax.all_to_all(terms, 'x', 0, 0, tiled=True)]
    all_to_all x2, starting transfers between devices: 17.4 us -> 10.4 us  [the longest x1 6.46 us: body(): terms = lax.all_to_all(terms, ('yh', 'yl'), 0, 0, tiled=True)]
    ppermute x7 -> x6, waiting for transfers between devices: 21.7 us -> 15.6 us  [swapped(): return lax.ppermute(value, axis, SWAP)]
    all_gather x2 -> x1, waiting for transfers between devices: 11.6 us -> 8.18 us  [body(): weights = lax.all_gather(weights, 'z', axis=0, tiled=False)]
    all_to_all x1, waiting for transfers between devices: 10 us -> 7.36 us  [to_everyone(): return lax.all_to_all(copies, axis, split_axis=0, concat_axis=0, tiled=True)]
    ppermute x7 -> x6, starting transfers between devices: 23.5 us -> 22.6 us  [swapped(): return lax.ppermute(value, axis, SWAP)]
    dot_general x4 -> x5, matrix products: 5.71 us -> 6.1 us  [the longest x2 5.49 us: down(): jnp.einsum('rh,zhk->zrk', hidden, weights, preferred_element_type=F32)]
  transfers between devices with their start and end apart: 12 -> 10, of which waited for: 10 -> 9; matrix products, arithmetic and copies ran while one was open for 6% -> 4% of each run, Pallas kernels for 0% -> 0%
where the time goes in v2:
time: 196 us; the launch traced here: 195 us
  blocking collectives  69 us (35%)
  waiting for transfers between devices  51.2 us (26%)
  starting transfers between devices  36.5 us (19%)
  between operations  14.4 us (7%)
  matrix products  10.2 us (5%)
  other arithmetic  7.13 us (4%)
  local copies, waits for them, and re-layouts  6.24 us (3%)
    all_to_all x1, blocking collectives, to_everyone(): return lax.all_to_all(copies, axis, split_axis=0, concat_axis=0, tiled=True)  40.4 us
    ppermute x6, starting transfers between devices, swapped(): return lax.ppermute(value, axis, SWAP)  22.6 us
    all_to_all x1, blocking collectives, body(): sums = lax.all_to_all(sums.reshape(32, 2, 384), LIST, 0, 0, tiled=True)  17.1 us
    ppermute x6, waiting for transfers between devices, swapped(): return lax.ppermute(value, axis, SWAP)  15.6 us
    all_to_all x1, blocking collectives, body(): blocks = lax.all_to_all(blocks, SHARD, 0, 0, tiled=True).reshape(128, 384)  11.6 us
    all_to_all x1, waiting for transfers between devices, body(): terms = lax.all_to_all(terms, 'x', 0, 0, tiled=True)  10.4 us
    all_to_all x1, waiting for transfers between devices, body(): terms = lax.all_to_all(terms, ('yh', 'yl'), 0, 0, tiled=True)  9.6 us
    all_gather x1, waiting for transfers between devices, body(): weights = lax.all_gather(weights, 'z', axis=0, tiled=False)  8.18 us
  transfers between devices with their start and end apart: 10, of which 9 were waited for; matrix products, arithmetic and copies ran while one was open for 4% of the time, Pallas kernels for 0%

profile of v2, /device:TPU:1, one launch (start us, length us, event | category | flops | bytes accessed | tf_op | source)
XLA Modules:
  0.0 194.7 jit_solution(568606931046287532)
XLA Ops:
  7.2 1.9 pad_maximum_fusion
  9.8 0.8 broadcast_select_fusion.5
  10.7 4.0 %collective-permute-start = (bf16[8,2176]{1,0:T(8,128)(2,1)S(1)}, bf16[8,2176]{1,0:T(8,128)(2,1)S(1)}, u32[]{:S(2)}, u32[]{:S(2)}) collective-permute-start(bf16[8,2176]{1,0:T(8,128)(2,1)S(1)} %pad_maximum_fusion.6), channel_id=1, source_target_pairs={{0,1},{1,0},{2,3},{3,2},{4,5},{5,4},{6,7},{7,6},{8,9},{9,8},{10,11... | collective-permute-start | bytes 104456 | tf_op jit(solution)/shard_map/ppermute | solution.py:15
  14.7 0.8 convert_element_type.92
  16.1 40.4 %all_to_all.30 = bf16[16,16,2304]{2,1,0:T(8,128)(2,1)S(1)} all-to-all(bf16[16,16,2304]{2,1,0:T(8,128)(2,1)S(1)} %broadcast_in_dim.14), channel_id=1, replica_groups=mesh['yh'=4,'x'=4,'c'=2,'z'=8,'yl'=2] {'x','yh'}, dimensions={0} | all-to-all | bytes 2359296 | tf_op jit(solution)/shard_map/all_to_all | solution.py:20
  56.5 4.5 %collective-permute-start.1 = (bf16[16,16,2304]{2,1,0:T(8,128)(2,1)S(1)}, bf16[16,16,2304]{2,1,0:T(8,128)(2,1)S(1)}, u32[]{:S(2)}, u32[]{:S(2)}) collective-permute-start(bf16[16,16,2304]{2,1,0:T(8,128)(2,1)S(1)} %all_to_all.30), channel_id=1, source_target_pairs={{0,16},{16,0},{1,17},{17,1},{2,18},{18,2},{3,19},{19,3},{4,20},{20... | collective-permute-start | bytes 3538952 | tf_op jit(solution)/shard_map/ppermute | solution.py:15
  61.0 2.5 %collective-permute-done.1 = bf16[16,16,2304]{2,1,0:T(8,128)(2,1)S(1)} collective-permute-done((bf16[16,16,2304]{2,1,0:T(8,128)(2,1)S(1)}, bf16[16,16,2304]{2,1,0:T(8,128)(2,1)S(1)}, u32[]{:S(2)}, u32[]{:S(2)}) %collective-permute-start.1) | collective-permute-done | bytes 1179680 | tf_op jit(solution)/shard_map/ppermute | solution.py:15
  64.5 1.2 copy.86
  65.7 8.2 %all-gather.3.cloned.1.call-done = bf16[8256,256]{1,0:T(8,128)(2,1)} async-done(((bf16[1032,256]{1,0:T(8,128)(2,1)}), bf16[8256,256]{1,0:T(8,128)(2,1)}) %all-gather.3.cloned.1.call-update) | async-done | bytes 4227088 | tf_op jit(solution)/shard_map/all_gather | solution.py:52
  73.9 3.2 %fusion.15 = bf16[256,688]{0,1:T(8,128)(2,1)S(1)} fusion(bf16[256,8,256]{2,0,1:T(8,128)(2,1)} %bitcast.89, bf16[8,1032,256]{2,1,0:T(8,128)(2,1)} %bitcast.110), kind=kOutput, calls=%fused_computation.17 | convolution fusion | flops 721596416 | bytes 4218880 | tf_op jit(solution)/shard_map/rzk,zhk->rh/dot_general | solution.py:38
  77.1 3.1 %collective-permute-start.2 = (bf16[256,688]{0,1:T(8,128)(2,1)S(1)}, bf16[256,688]{0,1:T(8,128)(2,1)S(1)}, u32[]{:S(2)}, u32[]{:S(2)}) collective-permute-start(bf16[256,688]{0,1:T(8,128)(2,1)S(1)} %fusion.15), channel_id=1, source_target_pairs={{0,1},{1,0},{2,3},{3,2},{4,5},{5,4},{6,7},{7,6},{8,9},{9,8},{10,11... | collective-permute-start | bytes 1056776 | tf_op jit(solution)/shard_map/ppermute | solution.py:15
  80.4 7.5 %collective-permute-done.2 = bf16[256,688]{0,1:T(8,128)(2,1)S(1)} collective-permute-done((bf16[256,688]{0,1:T(8,128)(2,1)S(1)}, bf16[256,688]{0,1:T(8,128)(2,1)S(1)}, u32[]{:S(2)}, u32[]{:S(2)}) %collective-permute-start.2) | collective-permute-done | bytes 352288 | tf_op jit(solution)/shard_map/ppermute | solution.py:15
  87.9 0.9 convert_add_fusion
  89.0 3.1 %collective-permute-start.3 = (bf16[256,344]{0,1:T(8,128)(2,1)S(1)}, bf16[256,344]{0,1:T(8,128)(2,1)S(1)}, u32[]{:S(2)}, u32[]{:S(2)}) collective-permute-start(bf16[256,344]{0,1:T(8,128)(2,1)S(1)} %fusion.18), channel_id=1, source_target_pairs={{0,1},{1,0},{2,3},{3,2},{4,5},{5,4},{6,7},{7,6},{8,9},{9,8},{10,11... | collective-permute-start | bytes 528392 | tf_op jit(solution)/shard_map/ppermute | solution.py:15
  92.3 2.9 %collective-permute-done.3 = bf16[256,344]{0,1:T(8,128)(2,1)S(1)} collective-permute-done((bf16[256,344]{0,1:T(8,128)(2,1)S(1)}, bf16[256,344]{0,1:T(8,128)(2,1)S(1)}, u32[]{:S(2)}, u32[]{:S(2)}) %collective-permute-start.3) | collective-permute-done | bytes 176160 | tf_op jit(solution)/shard_map/ppermute | solution.py:15
  95.5 3.1 %fusion.6 = bf16[8,256,256]{2,1,0:T(8,128)(2,1)} fusion(bf16[256,344,1]{1,0,2:T(8,128)(2,1)S(1)} %bitcast.99, bf16[8,1032,256]{2,1,0:T(8,128)(2,1)} %bitcast.111), kind=kOutput, calls=%fused_computation.12 | convolution fusion | flops 361234432 | bytes 2633728 | tf_op jit(solution)/shard_map/rh,zhk->zrk/dot_general | solution.py:42
  98.5 4.7 %collective-permute-start.4 = (bf16[8,256,256]{2,1,0:T(8,128)(2,1)}, bf16[8,256,256]{2,1,0:T(8,128)(2,1)}, u32[]{:S(2)}, u32[]{:S(2)}) collective-permute-start(bf16[8,256,256]{2,1,0:T(8,128)(2,1)} %fusion.6), channel_id=1, source_target_pairs={{0,16},{16,0},{1,17},{17,1},{2,18},{18,2},{3,19},{19,3},{4,20},{20... | collective-permute-start | bytes 3145736 | tf_op jit(solution)/shard_map/ppermute | solution.py:15
  103.6 2.3 %collective-permute-done.4 = bf16[8,256,256]{2,1,0:T(8,128)(2,1)} collective-permute-done((bf16[8,256,256]{2,1,0:T(8,128)(2,1)}, bf16[8,256,256]{2,1,0:T(8,128)(2,1)}, u32[]{:S(2)}, u32[]{:S(2)}) %collective-permute-start.4) | collective-permute-done | bytes 1048608 | tf_op jit(solution)/shard_map/ppermute | solution.py:15
  105.9 2.4 %fusion.5 = bf16[8,256,256]{2,1,0:T(8,128)(2,1)S(1)} fusion(bf16[8,256,256]{2,1,0:T(8,128)(2,1)} %collective-permute-done.4, bf16[256,344,1]{1,0,2:T(8,128)(2,1)S(1)} %bitcast.98, bf16[8,1032,256]{2,1,0:T(8,128)(2,1)} %bitcast.112), kind=kOutput, calls=%fused_computation.10 | convolution fusion | flops 362283008 | bytes 3682304 | tf_op jit(solution)/shard_map/rh,zhk->zrk/dot_general | solution.py:42
  108.3 1.1 copy.110
  109.4 4.0 %all-to-all-start.1 = ((bf16[4,8,64,256]{3,2,1,0:T(8,128)(2,1)}), bf16[4,8,64,256]{3,2,1,0:T(8,128)(2,1)S(1)}, u32[]{:S(2)}, u32[]{:S(2)}) async-start(bf16[4,8,64,256]{3,2,1,0:T(8,128)(2,1)} %bitcast.79), calls=%async_computation.1 | async-start | bytes 2097152 | tf_op jit(solution)/shard_map/all_to_all | solution.py:88
  114.2 3.1 %collective-permute-start.5 = (bf16[8,2048]{1,0:T(8,128)(2,1)S(1)}, bf16[8,2048]{1,0:T(8,128)(2,1)S(1)}, u32[]{:S(2)}, u32[]{:S(2)}) collective-permute-start(bf16[8,2048]{1,0:T(8,128)(2,1)S(1)} %convolution_convert_fusion), channel_id=1, source_target_pairs={{0,1},{1,0},{2,3},{3,2},{4,5},{5,4},{6,7},{7,6},{8,9},{9,8},{10,11... | collective-permute-start | bytes 98312 | tf_op jit(solution)/shard_map/ppermute | solution.py:15
  117.5 10.4 %all-to-all-done.1 = bf16[4,8,64,256]{3,2,1,0:T(8,128)(2,1)S(1)} async-done(((bf16[4,8,64,256]{3,2,1,0:T(8,128)(2,1)}), bf16[4,8,64,256]{3,2,1,0:T(8,128)(2,1)S(1)}, u32[]{:S(2)}, u32[]{:S(2)}) %all-to-all-start.1) | async-done | bytes 1048608 | tf_op jit(solution)/shard_map/all_to_all | solution.py:88
  128.2 0.7 copy.95
  128.9 6.5 %all-to-all-start.2 = ((bf16[8,8,8,256]{3,2,1,0:T(8,128)(2,1)}), bf16[8,8,8,256]{3,2,1,0:T(8,128)(2,1)S(1)}, u32[]{:S(2)}, u32[]{:S(2)}) async-start(bf16[8,8,8,256]{3,2,1,0:T(8,128)(2,1)} %bitcast.25), calls=%async_computation.2 | async-start | bytes 524288 | tf_op jit(solution)/shard_map/all_to_all | solution.py:92
  135.4 9.6 %all-to-all-done.2 = bf16[8,8,8,256]{3,2,1,0:T(8,128)(2,1)S(1)} async-done(((bf16[8,8,8,256]{3,2,1,0:T(8,128)(2,1)}), bf16[8,8,8,256]{3,2,1,0:T(8,128)(2,1)S(1)}, u32[]{:S(2)}, u32[]{:S(2)}) %all-to-all-start.2) | async-done | bytes 262176 | tf_op jit(solution)/shard_map/all_to_all | solution.py:92
  145.4 0.7 multiply_convert_fusion
  146.2 11.6 %all_to_all.31 = bf16[16,8,384]{2,1,0:T(8,128)(2,1)S(1)} all-to-all(bf16[16,8,384]{2,1,0:T(8,128)(2,1)S(1)} %pad_maximum_fusion.3), channel_id=1, replica_groups=mesh['yh'=4,'x'=4,'c'=2,'z'=8,'yl'=2] {'z','yl'}, dimensions={0} | all-to-all | bytes 196608 | tf_op jit(solution)/shard_map/all_to_all | solution.py:104
  158.5 17.1 %all_to_all.32 = bf16[32,2,384]{2,1,0:T(2,128)(2,1)S(1)} all-to-all(bf16[32,2,384]{2,1,0:T(2,128)(2,1)S(1)} %reshape.91), channel_id=1, replica_groups=mesh['yh'=4,'x'=4,'c'=2,'z'=8,'yl'=2] {'yh','x','c'}, dimensions={0} | all-to-all | bytes 98304 | tf_op jit(solution)/shard_map/all_to_all | solution.py:109
  176.2 3.5 %all-to-all-start.5 = ((f32[16,2,256]{2,1,0:T(2,128)}), f32[16,2,256]{2,1,0:T(2,128)S(1)}, u32[]{:S(2)}, u32[]{:S(2)}) async-start(f32[16,2,256]{2,1,0:T(2,128)} %broadcast_in_dim.16), calls=%async_computation.5 | async-start | bytes 65536 | tf_op jit(solution)/shard_map/all_to_all | solution.py:20
  179.8 7.4 %all-to-all-done.5 = f32[16,2,256]{2,1,0:T(2,128)S(1)} async-done(((f32[16,2,256]{2,1,0:T(2,128)}), f32[16,2,256]{2,1,0:T(2,128)S(1)}, u32[]{:S(2)}, u32[]{:S(2)}) %all-to-all-start.5) | async-done | bytes 32800 | tf_op jit(solution)/shard_map/all_to_all | solution.py:20
  187.2 0.7 add_divide_fusion
  (68 shorter events, 6.6 us)
Async XLA Ops:
  7.2 66.7 %all-gather.3.cloned.1.call-start = ((), (), s32[]{:S(2)}) async-start(), calls=%async_computation.6 | async-start | bytes 4755456 | tf_op jit(solution)/shard_map/all_gather | solution.py:52
  10.7 5.3 %collective-permute-start = (bf16[8,2176]{1,0:T(8,128)(2,1)S(1)}, bf16[8,2176]{1,0:T(8,128)(2,1)S(1)}, u32[]{:S(2)}, u32[]{:S(2)}) collective-permute-start(bf16[8,2176]{1,0:T(8,128)(2,1)S(1)} %pad_maximum_fusion.6), channel_id=1, source_target_pairs={{0,1},{1,0},{2,3},{3,2},{4,5},{5,4},{6,7},{7,6},{8,9},{9,8},{10,11... | collective-permute-start | bytes 104456 | tf_op jit(solution)/shard_map/ppermute | solution.py:15
  56.5 6.9 %collective-permute-start.1 = (bf16[16,16,2304]{2,1,0:T(8,128)(2,1)S(1)}, bf16[16,16,2304]{2,1,0:T(8,128)(2,1)S(1)}, u32[]{:S(2)}, u32[]{:S(2)}) collective-permute-start(bf16[16,16,2304]{2,1,0:T(8,128)(2,1)S(1)} %all_to_all.30), channel_id=1, source_target_pairs={{0,16},{16,0},{1,17},{17,1},{2,18},{18,2},{3,19},{19,3},{4,20},{20... | collective-permute-start | bytes 3538952 | tf_op jit(solution)/shard_map/ppermute | solution.py:15
  73.9 14.0 %slice-start = ((s8[4227072]{0:T(1024)(128)(4,1)}), s8[4194304]{0:T(1024)(128)(4,1)S(1)}, s32[]{:S(2)}) async-start(s8[4227072]{0:T(1024)(128)(4,1)} %bitcast.113), calls=%async_computation.7 | async-start | bytes 8388608
  73.9 14.0 %slice-start.1 = ((s8[4227072]{0:T(1024)(128)(4,1)}), s8[32768]{0:T(1024)(128)(4,1)S(1)}, s32[]{:S(2)}) async-start(s8[4227072]{0:T(1024)(128)(4,1)} %bitcast.113), calls=%async_computation.8 | async-start | bytes 65536
  77.1 10.8 %collective-permute-start.2 = (bf16[256,688]{0,1:T(8,128)(2,1)S(1)}, bf16[256,688]{0,1:T(8,128)(2,1)S(1)}, u32[]{:S(2)}, u32[]{:S(2)}) collective-permute-start(bf16[256,688]{0,1:T(8,128)(2,1)S(1)} %fusion.15), channel_id=1, source_target_pairs={{0,1},{1,0},{2,3},{3,2},{4,5},{5,4},{6,7},{7,6},{8,9},{9,8},{10,11... | collective-permute-start | bytes 1056776 | tf_op jit(solution)/shard_map/ppermute | solution.py:15
  89.0 6.2 %collective-permute-start.3 = (bf16[256,344]{0,1:T(8,128)(2,1)S(1)}, bf16[256,344]{0,1:T(8,128)(2,1)S(1)}, u32[]{:S(2)}, u32[]{:S(2)}) collective-permute-start(bf16[256,344]{0,1:T(8,128)(2,1)S(1)} %fusion.18), channel_id=1, source_target_pairs={{0,1},{1,0},{2,3},{3,2},{4,5},{5,4},{6,7},{7,6},{8,9},{9,8},{10,11... | collective-permute-start | bytes 528392 | tf_op jit(solution)/shard_map/ppermute | solution.py:15
  95.3 8.0 %copy-start.3 = (s32[8]{0:T(128)S(1)}, s32[8]{0:T(128)}, u32[]{:S(2)}) copy-start(s32[8]{0:T(128)} %param.15) | copy-start | bytes 100
  98.5 7.4 %collective-permute-start.4 = (bf16[8,256,256]{2,1,0:T(8,128)(2,1)}, bf16[8,256,256]{2,1,0:T(8,128)(2,1)}, u32[]{:S(2)}, u32[]{:S(2)}) collective-permute-start(bf16[8,256,256]{2,1,0:T(8,128)(2,1)} %fusion.6), channel_id=1, source_target_pairs={{0,16},{16,0},{1,17},{17,1},{2,18},{18,2},{3,19},{19,3},{4,20},{20... | collective-permute-start | bytes 3145736 | tf_op jit(solution)/shard_map/ppermute | solution.py:15
  109.4 18.5 %all-to-all-start.1 = ((bf16[4,8,64,256]{3,2,1,0:T(8,128)(2,1)}), bf16[4,8,64,256]{3,2,1,0:T(8,128)(2,1)S(1)}, u32[]{:S(2)}, u32[]{:S(2)}) async-start(bf16[4,8,64,256]{3,2,1,0:T(8,128)(2,1)} %bitcast.79), calls=%async_computation.1 | async-start | bytes 2097152 | tf_op jit(solution)/shard_map/all_to_all | solution.py:88
  114.2 21.2 %collective-permute-start.5 = (bf16[8,2048]{1,0:T(8,128)(2,1)S(1)}, bf16[8,2048]{1,0:T(8,128)(2,1)S(1)}, u32[]{:S(2)}, u32[]{:S(2)}) collective-permute-start(bf16[8,2048]{1,0:T(8,128)(2,1)S(1)} %convolution_convert_fusion), channel_id=1, source_target_pairs={{0,1},{1,0},{2,3},{3,2},{4,5},{5,4},{6,7},{7,6},{8,9},{9,8},{10,11... | collective-permute-start | bytes 98312 | tf_op jit(solution)/shard_map/ppermute | solution.py:15
  117.5 27.8 %copy-start = (bf16[8,4096]{1,0:T(8,128)(2,1)S(1)}, bf16[8,4096]{1,0:T(8,128)(2,1)}, u32[]{:S(2)}) copy-start(bf16[8,4096]{1,0:T(8,128)(2,1)} %param.8) | copy-start | bytes 196612
  117.5 27.9 %copy-start.2 = (f32[4096]{0:T(1024)S(1)}, f32[4096]{0:T(1024)}, u32[]{:S(2)}) copy-start(f32[4096]{0:T(1024)} %param.9) | copy-start | bytes 49156
  128.2 59.0 %copy-start.1 = (f32[2,4096]{1,0:T(2,128)S(1)}, f32[2,4096]{1,0:T(2,128)}, u32[]{:S(2)}) copy-start(f32[2,4096]{1,0:T(2,128)} %param.13) | copy-start | bytes 98308
  128.9 16.1 %all-to-all-start.2 = ((bf16[8,8,8,256]{3,2,1,0:T(8,128)(2,1)}), bf16[8,8,8,256]{3,2,1,0:T(8,128)(2,1)S(1)}, u32[]{:S(2)}, u32[]{:S(2)}) async-start(bf16[8,8,8,256]{3,2,1,0:T(8,128)(2,1)} %bitcast.25), calls=%async_computation.2 | async-start | bytes 524288 | tf_op jit(solution)/shard_map/all_to_all | solution.py:92
  176.2 11.0 %all-to-all-start.5 = ((f32[16,2,256]{2,1,0:T(2,128)}), f32[16,2,256]{2,1,0:T(2,128)S(1)}, u32[]{:S(2)}, u32[]{:S(2)}) async-start(f32[16,2,256]{2,1,0:T(2,128)} %broadcast_in_dim.16), calls=%async_computation.5 | async-start | bytes 65536 | tf_op jit(solution)/shard_map/all_to_all | solution.py:20
Sparse Core Ops, SparseCore 0:
  10.1 63.7 all-gather.2
